TPU v7x, 32 devices: a whole 2x2x4 slice. The times are simulated.
32 devices in a mesh: attn: 4 (over y, x), expert: 8 (over z, core).
Axes of the slice: x: 2, y: 2, z: 4, core: 2. Of those that a mesh axis runs over, the one named last changes fastest.
Arguments:
- tokens: bfloat16 [1024, 2880], P(('attn', 'expert')), may hold values from -6 to 6
- expert_ids: int32 [1024, 4], P(('attn', 'expert')), may hold values from 0 to 7, all different within a row; in each aligned block of 32 rows (0 to 31, 32 to 63, ...) at most 32 rows name the same one
- gate_probs: float32 [1024, 4], P(('attn', 'expert')), may hold values from 0.05 to 0.6
- shed_blocks: int32 [8], replicated, may hold values from 0 to 4, as said below
- partner: int32 [8], replicated, may hold values from 0 to 7, as said below
- gate_weight: bfloat16 [8, 2880, 2880], P('expert', None, 'attn'), may hold values from -0.109375 to 0.109375
- up_weight: bfloat16 [8, 2880, 2880], P('expert', None, 'attn'), may hold values from -0.109375 to 0.109375
- down_weight: bfloat16 [8, 2880, 2880], P('expert', 'attn'), may hold values from -0.109375 to 0.109375
Outputs:
- moe_out: bfloat16 [1024, 2880], P(('attn', 'expert'))
Inputs may be any that keep to these rules, and one draw needn't show every extreme that they name: `expert_ids`: in the rows of one device, no expert is named by more than 32 rows; the 4 experts of a token differ. `shed_blocks`: some expert has exactly 4. partner pairs the experts: partner[partner[e]] = e and partner[e] != e.
All inputs are finite; a program needn't handle non-finite values.
Results may differ from a plain program's by a relative error of at most 0.0081.
Values may be sent and summed in bfloat16 or wider, within the bound.
A program may use at most 128 MiB of HBM per device.

v0:
```python
import jax
import jax.numpy as jnp
from jax import lax
from jax.sharding import PartitionSpec as P

SHED_MOST = 4
SWISH_SCALE = 1.702


def lookup(table, indices):
    places = jnp.arange(table.shape[0], dtype=jnp.int32)
    return jnp.sum(jnp.where(indices[:, None] == places[None, :], table[None, :], 0), axis=1)


def activate(rows, gate_w, up_w):
    gate_part = jnp.dot(rows, gate_w, preferred_element_type=jnp.float32)
    up_part = jnp.dot(rows, up_w, preferred_element_type=jnp.float32)
    return (gate_part * jax.nn.sigmoid(SWISH_SCALE * gate_part) * (up_part + 1.0)).astype(
        jnp.bfloat16
    )


def on_device(
    tokens, expert_ids, gate_probs, shed_blocks, partner, gate_weight, up_weight, down_weight
):
    tok_rows, model_width = tokens.shape
    top_count = expert_ids.shape[1]
    expert_count = shed_blocks.shape[0]
    group_count = lax.axis_size("attn")
    capacity = tok_rows * top_count * group_count
    block_size = capacity // 8
    most_rows = min(tok_rows, 3 * tok_rows * top_count // expert_count)
    slot_count = 2 * most_rows
    places = jnp.arange(expert_count, dtype=jnp.int32)
    flat_ids = expert_ids.reshape(-1)
    onehot = (flat_ids[:, None] == places[None, :]).astype(jnp.int32)
    counts = jnp.sum(onehot, axis=0)
    local_rank = jnp.sum((jnp.cumsum(onehot, axis=0) - onehot) * onehot, axis=1)
    everyone = lax.all_gather(counts[None, :], ("attn", "expert"), axis=0, tiled=True)
    position_now = lax.axis_index(("attn", "expert"))
    earlier = (jnp.arange(everyone.shape[0], dtype=jnp.int32) < position_now)[:, None]
    offsets = jnp.sum(jnp.where(earlier, everyone, 0), axis=0)
    global_rank = local_rank + jnp.sum(onehot * offsets[None, :], axis=1)
    limit = capacity - block_size * lookup(shed_blocks, partner)
    own_limit = lookup(limit, flat_ids)
    own_shed = lookup(shed_blocks, flat_ids)
    native = global_rank < own_limit
    borrowed = jnp.logical_and(
        jnp.logical_not(native), global_rank < own_limit + block_size * own_shed
    )
    usable = jnp.logical_or(native, borrowed)
    target = jnp.where(usable, flat_ids, -1)
    table_rows = capacity + block_size * SHED_MOST
    target_hot = (target[:, None] == places[None, :]).astype(jnp.int32)
    position = jnp.sum((jnp.cumsum(target_hot, axis=0) - target_hot) * target_hot, axis=1)
    buffer_index = jnp.where(usable, target * slot_count + position, expert_count * slot_count)
    token_rows = jnp.repeat(tokens, top_count, axis=0)
    send_rows = (
        jnp.zeros((expert_count * slot_count, model_width), jnp.bfloat16)
        .at[buffer_index]
        .set(token_rows, mode="drop")
    )
    send_slots = (
        jnp.full((expert_count * slot_count,), table_rows, jnp.int32)
        .at[buffer_index]
        .set(global_rank, mode="drop")
    )
    send_rows = send_rows.reshape(expert_count, slot_count, model_width)
    send_slots = send_slots.reshape(expert_count, slot_count)
    got_rows, got_slots = (
        lax.all_to_all(send_rows, "expert", split_axis=0, concat_axis=0, tiled=True),
        lax.all_to_all(send_slots, "expert", split_axis=0, concat_axis=0, tiled=True),
    )
    local_table = (
        jnp.zeros((table_rows, model_width), jnp.float32)
        .at[got_slots.reshape(-1)]
        .set(got_rows.reshape(-1, model_width).astype(jnp.float32), mode="drop")
    )
    compact = lax.psum(local_table.astype(jnp.bfloat16), "attn")
    gate_own = gate_weight[0]
    up_own = up_weight[0]
    down_own = down_weight[0]
    hidden_own = activate(compact, gate_own, up_own)
    share = lax.psum_scatter(
        jnp.dot(hidden_own, down_own, preferred_element_type=jnp.float32),
        "attn",
        scatter_dimension=0,
        tiled=True,
    )
    results = lax.all_gather(share.astype(jnp.bfloat16), "attn", axis=0, tiled=True)
    answers = results[jnp.minimum(got_slots, table_rows - 1)]
    returned = lax.all_to_all(answers, "expert", split_axis=0, concat_axis=0, tiled=True)
    flat_back = returned.reshape(expert_count * slot_count, model_width)
    picked = flat_back[jnp.minimum(buffer_index, expert_count * slot_count - 1)]
    weights = jnp.where(usable, gate_probs.reshape(-1), 0.0)
    mixed = picked.astype(jnp.float32) * weights[:, None]
    return mixed.reshape(tok_rows, top_count, model_width).sum(axis=1).astype(jnp.bfloat16)


def solution(mesh):
    in_specs = (
        P(("attn", "expert"), None),
        P(("attn", "expert"), None),
        P(("attn", "expert"), None),
        P(),
        P(),
        P("expert", None, "attn"),
        P("expert", None, "attn"),
        P("expert", "attn", None),
    )
    out_specs = P(("attn", "expert"), None)
    return jax.shard_map(
        on_device, mesh=mesh, in_specs=in_specs, out_specs=out_specs, check_vma=False
    )
```

profile of v0, /device:TPU:0, one launch (start us, length us, event | category | flops | bytes accessed | tf_op | source)
XLA Modules:
  0.0 529.1 jit_solution(730793958750302019)
XLA Ops:
  6.5 0.8 copy.15
  7.3 0.1 eq.20
  7.4 0.1 fusion.17
  7.5 0.1 fusion.16
  7.6 0.1 reshape.235
  7.7 0.2 dynamic-update-slice
  8.0 42.0 %all-reduce = s32[256]{0:T(256)S(1)} all-reduce(s32[256]{0:T(256)S(1)} %dynamic-update-slice), channel_id=2, replica_groups=mesh['attn'=4,'expert'=8] {'attn','expert'}, use_global_device_ids=true, to_apply=%add | all-reduce | flops 256 | bytes 2048
  49.9 0.1 reshape.282
  50.0 0.2 reduce_window_sum.17
  50.2 0.9 select_reduce_fusion.6
  51.1 0.1 select_reduce_fusion.5
  51.1 0.9 select_reduce_fusion.1
  52.0 0.1 fusion.15
  52.1 0.2 reduce_window_sum.18
  52.3 0.2 select_reduce_fusion
  52.5 1.0 scatter_custom_fusion
  53.5 0.7 all_to_all.12
  54.2 3.6 all-to-all-start
  57.8 1.1 broadcast_in_dim.95
  58.9 0.4 reshape.270
  59.3 3.8 scatter_custom_fusion.1
  63.0 0.2 all-to-all-done
  63.3 4.9 all-to-all-start.1
  68.2 0.0 all-reduce.3.cloned.1.call-start
  68.2 0.5 broadcast.220
  68.7 0.7 broadcast_minimum_fusion
  69.4 0.1 reshape.236
  69.5 67.4 %all-to-all-done.1 = bf16[8,64,2880]{2,1,0:T(8,128)(2,1)S(1)} async-done(((bf16[8,64,2880]{2,1,0:T(8,128)(2,1)}), bf16[8,64,2880]{2,1,0:T(8,128)(2,1)S(1)}, u32[]{:S(2)}, u32[]{:S(2)}) %all-to-all-start.1) | async-done | bytes 2949152 | tf_op jit(solution)/shard_map/all_to_all | solution.py:71
  136.8 8.4 %scatter_custom_fusion.2 = f32[768,2880]{1,0:T(8,128)} fusion(s32[512]{0:T(512)S(1)} %bitcast.54, bf16[512,2880]{1,0:T(8,128)(2,1)S(1)} %bitcast.51, f32[]{:T(128)} %constant.14.clone.1), kind=kCustom, calls=%fused_computation.5 | custom fusion | flops 1474560 | bytes 11862020 | tf_op jit(solution)/shard_map/scatter | solution.py:77
  145.3 6.1 %convert_element_type.35 = bf16[768,2880]{1,0:T(8,128)(2,1)} convert(f32[768,2880]{1,0:T(8,128)} %scatter_custom_fusion.2) | non-fusion elementwise | flops 2211840 | bytes 13271040 | tf_op jit(solution)/shard_map/convert_element_type | solution.py:79
  151.3 0.0 all-reduce.3.cloned.1.call-update
  151.4 0.2 reduce-scatter.2.cloned.1.call-start
  151.6 107.7 %all-reduce.3.cloned.1.call-done = bf16[768,2880]{1,0:T(8,128)(2,1)} async-done(((bf16[768,2880]{1,0:T(8,128)(2,1)}), bf16[768,2880]{1,0:T(8,128)(2,1)}) %all-reduce.3.cloned.1.call-update) | async-done | bytes 4423696 | tf_op jit(solution)/shard_map/psum | solution.py:79
  259.3 6.8 %fusion.5 = f32[768,720]{0,1:T(8,128)S(1)} fusion(bf16[768,2880]{1,0:T(8,128)(2,1)} %all-reduce.3.cloned.1.call-done, bf16[1,2880,720]{1,2,0:T(8,128)(2,1)} %param.14), kind=kOutput, calls=%fused_computation.10 | convolution fusion | flops 3185049600 | bytes 10782720 | tf_op jit(solution)/shard_map/dot_general | solution.py:17
  266.1 18.0 %fusion.3 = f32[768,2880]{1,0:T(8,128)} fusion(bf16[1,720,2880]{2,1,0:T(8,128)(2,1)} %param.15, f32[768,720]{0,1:T(8,128)S(1)} %fusion.5, bf16[768,2880]{1,0:T(8,128)(2,1)} %all-reduce.3.cloned.1.call-done, bf16[1,2880,720]{1,2,0:T(8,128)(2,1)} %param.13), kind=kOutput, calls=%fused_computation.8 | convolution fusion | flops 6374522880 | bytes 23777280 | tf_op jit(solution)/shard_map/dot_general | solution.py:85
  284.1 0.0 reduce-scatter.2.cloned.1.call-update
  284.1 0.3 all-gather.3.cloned.1.call-start
  284.4 91.6 %reduce-scatter.2.cloned.1.call-done = f32[192,2880]{1,0:T(8,128)} async-done(((f32[768,2880]{1,0:T(8,128)}), f32[192,2880]{1,0:T(8,128)}) %reduce-scatter.2.cloned.1.call-update) | async-done | bytes 2211856 | tf_op jit(solution)/shard_map/reduce_scatter | solution.py:84
  376.0 2.8 convert_element_type.37
  378.8 0.0 all-gather.3.cloned.1.call-update
  378.8 0.1 reshape.244
  378.9 55.4 %all-gather.3.cloned.1.call-done = bf16[768,2880]{1,0:T(8,128)(2,1)} async-done(((bf16[192,2880]{1,0:T(8,128)(2,1)}), bf16[768,2880]{1,0:T(8,128)(2,1)}) %all-gather.3.cloned.1.call-update) | async-done | bytes 4423696 | tf_op jit(solution)/shard_map/all_gather | solution.py:90
  434.2 9.6 %gather_fusion = bf16[512,2880]{1,0:T(8,128)(2,1)} fusion(bf16[768,2880]{1,0:T(8,128)(2,1)} %all-gather.3.cloned.1.call-done, s32[1024]{0:T(1024)S(1)} %pad_clamp_fusion.1), kind=kCustom, calls=%fused_computation | custom fusion | bytes 5900288 | tf_op jit(solution)/shard_map/gather | solution.py:91
  443.8 0.0 copy-start
  443.8 4.7 all-to-all-start.2
  448.6 0.1 add.134
  448.7 0.1 reduce_sum.97
  448.8 0.1 mul.98
  448.9 0.0 copy-done
  448.9 0.1 copy.17
  449.0 68.3 %all-to-all-done.2 = bf16[8,64,2880]{2,1,0:T(8,128)(2,1)S(1)} async-done(((bf16[8,64,2880]{2,1,0:T(8,128)(2,1)}), bf16[8,64,2880]{2,1,0:T(8,128)(2,1)S(1)}, u32[]{:S(2)}, u32[]{:S(2)}) %all-to-all-start.2) | async-done | bytes 2949152 | tf_op jit(solution)/shard_map/all_to_all | solution.py:92
  517.3 1.9 gather_fusion.1
  519.2 1.7 reshape.241
  520.8 1.7 multiply_reduce_fusion
  (11 shorter events, 0.1 us)
Async XLA Ops:
  54.2 9.1 %all-to-all-start = ((s32[8,1,64]{2,1,0:T(1,128)}), s32[8,1,64]{2,1,0:T(1,128)S(1)}, u32[]{:S(2)}, u32[]{:S(2)}) async-start(s32[8,1,64]{2,1,0:T(1,128)} %all_to_all.12), calls=%async_computation | async-start | bytes 8192 | tf_op jit(solution)/shard_map/all_to_all | solution.py:72
  63.3 73.6 %all-to-all-start.1 = ((bf16[8,64,2880]{2,1,0:T(8,128)(2,1)}), bf16[8,64,2880]{2,1,0:T(8,128)(2,1)S(1)}, u32[]{:S(2)}, u32[]{:S(2)}) async-start(bf16[8,64,2880]{2,1,0:T(8,128)(2,1)} %bitcast.6), calls=%async_computation.1 | async-start | bytes 6029312 | tf_op jit(solution)/shard_map/all_to_all | solution.py:71
  68.2 191.2 %all-reduce.3.cloned.1.call-start = ((), (), s32[]{:S(2)}) async-start(), calls=%async_computation.4 | async-start | bytes 9043968 | tf_op jit(solution)/shard_map/psum | solution.py:79
  151.4 224.6 %reduce-scatter.2.cloned.1.call-start = ((), (), s32[]{:S(2)}) async-start(), calls=%async_computation.5 | async-start | bytes 11304960 | tf_op jit(solution)/shard_map/reduce_scatter | solution.py:84
  284.1 150.1 %all-gather.3.cloned.1.call-start = ((), (), s32[]{:S(2)}) async-start(), calls=%async_computation.6 | async-start | bytes 5652480 | tf_op jit(solution)/shard_map/all_gather | solution.py:90
  443.8 5.1 copy-start
  443.8 73.4 %all-to-all-start.2 = ((bf16[8,64,2880]{2,1,0:T(8,128)(2,1)}), bf16[8,64,2880]{2,1,0:T(8,128)(2,1)S(1)}, u32[]{:S(2)}, u32[]{:S(2)}) async-start(bf16[8,64,2880]{2,1,0:T(8,128)(2,1)} %bitcast.52), calls=%async_computation.3 | async-start | bytes 6029312 | tf_op jit(solution)/shard_map/all_to_all | solution.py:92
Sparse Core Ops, SparseCore 0:
  151.5 107.7 all-reduce.2
  284.3 91.6 reduce-scatter.1
  378.9 55.2 all-gather.2
where the time goes:
time: 530 us; the launch traced here: 529 us
  waiting for transfers between devices  391 us (74%)
  blocking collectives  42 us (8%)
  matrix products  24.8 us (5%)
  local copies, waits for them, and re-layouts  22.4 us (4%)
  other arithmetic  22.3 us (4%)
  starting transfers between devices  13.7 us (3%)
  between operations  13.3 us (3%)
    psum x1, waiting for transfers between devices, on_device(): compact = lax.psum(local_table.astype(jnp.bfloat16), 'attn')  108 us
    reduce_scatter x1, waiting for transfers between devices, on_device(): lax.psum_scatter(jnp.dot(hidden_own, down_own, preferred_element_type=jnp...  91.6 us
    all_to_all x1, waiting for transfers between devices, on_device(): lax.all_to_all(answers, 'expert', split_axis=0, concat_axis=0, tiled=True)  68.3 us
    all_to_all x1, waiting for transfers between devices, on_device(): lax.all_to_all(send_rows, 'expert', split_axis=0, concat_axis=0, tiled=True)  67.4 us
    all_gather x1, waiting for transfers between devices, on_device(): lax.all_gather(share.astype(jnp.bfloat16), 'attn', axis=0, tiled=True)  55.4 us
    unnamed x1, blocking collectives  42 us
    dot_general x1, matrix products, on_device(): jnp.dot(hidden_own, down_own, preferred_element_type=jnp.float32)  18 us
  transfers between devices with their start and end apart: 6, of which 6 were waited for; matrix products, arithmetic and copies ran while one was open for 1% of the time, Pallas kernels for 0%

commit v1 on v0

--- a/solution.py
+++ b/solution.py
@@ -76,7 +76,7 @@
         .at[got_slots.reshape(-1)]
         .set(got_rows.reshape(-1, model_width).astype(jnp.float32), mode="drop")
     )
-    compact = lax.psum(local_table.astype(jnp.bfloat16), "attn")
+    compact = jnp.sum(lax.all_gather(local_table.astype(jnp.bfloat16), "attn"), axis=0)
     gate_own = gate_weight[0]
     up_own = up_weight[0]
     down_own = down_weight[0]

time: 530 us -> 602 us (1.14)
  waiting for transfers between devices: 391 us -> 451 us
  other arithmetic: 22.3 us -> 34.7 us
    all_gather x0 -> x1, waiting for transfers between devices: none -> 168 us  [on_device(): lax.all_gather(local_table.astype(jnp.bfloat16), 'attn')]
    psum x1 -> x0, waiting for transfers between devices: 108 us -> none  [on_device(): compact = lax.psum(local_table.astype(jnp.bfloat16), 'attn')]
    unnamed x0 -> x1, other arithmetic: none -> 12.4 us
where the time goes in v1:
time: 602 us
  waiting for transfers between devices  451 us (75%)
  blocking collectives  42 us (7%)
  other arithmetic  34.7 us (6%)
  matrix products  24.8 us (4%)
  local copies, waits for them, and re-layouts  22.4 us (4%)
  starting transfers between devices  13.7 us (2%)
  between operations  13.3 us (2%)
    all_gather x1, waiting for transfers between devices, on_device(): lax.all_gather(local_table.astype(jnp.bfloat16), 'attn')  168 us
    reduce_scatter x1, waiting for transfers between devices, on_device(): lax.psum_scatter(jnp.dot(hidden_own, down_own, preferred_element_type=jnp...  91.6 us
    all_to_all x1, waiting for transfers between devices, on_device(): lax.all_to_all(answers, 'expert', split_axis=0, concat_axis=0, tiled=True)  68.3 us
    all_to_all x1, waiting for transfers between devices, on_device(): lax.all_to_all(send_rows, 'expert', split_axis=0, concat_axis=0, tiled=True)  67.4 us
    all_gather x1, waiting for transfers between devices, on_device(): lax.all_gather(share.astype(jnp.bfloat16), 'attn', axis=0, tiled=True)  55.4 us
    unnamed x1, blocking collectives  42 us
    dot_general x1, matrix products, on_device(): jnp.dot(hidden_own, down_own, preferred_element_type=jnp.float32)  18 us
    unnamed x1, other arithmetic  12.4 us
  transfers between devices with their start and end apart: 6, of which 6 were waited for; matrix products, arithmetic and copies ran while one was open for 1% of the time, Pallas kernels for 0%

profile of v1, /device:TPU:0, one launch (start us, length us, event | category | flops | bytes accessed | tf_op | source)
XLA Modules:
  0.0 601.8 jit_solution(9270770664053945203)
XLA Ops:
  6.5 0.8 copy.18
  7.3 0.1 eq.20
  7.4 0.1 fusion.17
  7.5 0.1 fusion.16
  7.6 0.1 reshape.235
  7.7 0.2 dynamic-update-slice
  8.0 42.0 %all-reduce = s32[256]{0:T(256)S(1)} all-reduce(s32[256]{0:T(256)S(1)} %dynamic-update-slice), channel_id=2, replica_groups=mesh['attn'=4,'expert'=8] {'attn','expert'}, use_global_device_ids=true, to_apply=%add | all-reduce | flops 256 | bytes 2048
  49.9 0.1 reshape.282
  50.0 0.2 reduce_window_sum.17
  50.2 0.9 select_reduce_fusion.6
  51.1 0.1 select_reduce_fusion.5
  51.2 0.9 select_reduce_fusion.1
  52.0 0.1 fusion.15
  52.1 0.2 reduce_window_sum.18
  52.3 0.2 select_reduce_fusion
  52.5 1.0 scatter_custom_fusion
  53.5 0.7 all_to_all.12
  54.2 3.6 all-to-all-start
  57.8 1.1 broadcast_in_dim.95
  58.9 0.4 reshape.270
  59.3 3.8 scatter_custom_fusion.1
  63.1 0.2 all-to-all-done
  63.3 4.9 all-to-all-start.1
  68.2 0.0 all-gather.7.cloned.1.call-start
  68.2 0.5 broadcast.220
  68.7 0.7 broadcast_minimum_fusion
  69.4 0.1 reshape.236
  69.5 67.4 %all-to-all-done.1 = bf16[8,64,2880]{2,1,0:T(8,128)(2,1)S(1)} async-done(((bf16[8,64,2880]{2,1,0:T(8,128)(2,1)}), bf16[8,64,2880]{2,1,0:T(8,128)(2,1)S(1)}, u32[]{:S(2)}, u32[]{:S(2)}) %all-to-all-start.1) | async-done | bytes 2949152 | tf_op jit(solution)/shard_map/all_to_all | solution.py:71
  136.8 8.4 %scatter_custom_fusion.2 = f32[768,2880]{1,0:T(8,128)} fusion(s32[512]{0:T(512)S(1)} %bitcast.56, bf16[512,2880]{1,0:T(8,128)(2,1)S(1)} %bitcast.53, f32[]{:T(128)} %constant.14.clone.1), kind=kCustom, calls=%fused_computation.5 | custom fusion | flops 1474560 | bytes 11862020 | tf_op jit(solution)/shard_map/scatter | solution.py:77
  145.3 6.1 %convert_element_type.37 = bf16[768,2880]{1,0:T(8,128)(2,1)} convert(f32[768,2880]{1,0:T(8,128)} %scatter_custom_fusion.2) | non-fusion elementwise | flops 2211840 | bytes 13271040 | tf_op jit(solution)/shard_map/convert_element_type | solution.py:79
  151.4 0.0 all-gather.7.cloned.1.call-update
  151.4 0.2 reduce-scatter.2.cloned.1.call-start
  151.7 168.0 %all-gather.7.cloned.1.call-done = bf16[3072,2880]{1,0:T(8,128)(2,1)} async-done(((bf16[768,2880]{1,0:T(8,128)(2,1)}), bf16[3072,2880]{1,0:T(8,128)(2,1)}) %all-gather.7.cloned.1.call-update) | async-done | bytes 17694736 | tf_op jit(solution)/shard_map/all_gather | solution.py:79
  319.7 12.4 %reduce_sum.109 = bf16[768,2880]{1,0:T(8,128)(2,1)} reduce(bf16[4,768,2880]{2,1,0:T(8,128)(2,1)} %bitcast.52, bf16[]{:T(256)} %constant.23.clone.1), dimensions={0}, to_apply=%region_13.14 | reduce | flops 6635520 | bytes 22118402
  332.0 6.8 %fusion.5 = f32[768,720]{0,1:T(8,128)S(1)} fusion(bf16[768,2880]{1,0:T(8,128)(2,1)} %reduce_sum.109, bf16[1,2880,720]{1,2,0:T(8,128)(2,1)} %param.14), kind=kOutput, calls=%fused_computation.10 | convolution fusion | flops 3185049600 | bytes 10782720 | tf_op jit(solution)/shard_map/dot_general | solution.py:17
  338.8 18.0 %fusion.3 = f32[768,2880]{1,0:T(8,128)} fusion(bf16[1,720,2880]{2,1,0:T(8,128)(2,1)} %param.15, f32[768,720]{0,1:T(8,128)S(1)} %fusion.5, bf16[768,2880]{1,0:T(8,128)(2,1)} %reduce_sum.109, bf16[1,2880,720]{1,2,0:T(8,128)(2,1)} %param.13), kind=kOutput, calls=%fused_computation.8 | convolution fusion | flops 6374522880 | bytes 23777280 | tf_op jit(solution)/shard_map/dot_general | solution.py:85
  356.9 0.0 reduce-scatter.2.cloned.1.call-update
  356.9 0.3 all-gather.5.cloned.1.call-start
  357.1 91.6 %reduce-scatter.2.cloned.1.call-done = f32[192,2880]{1,0:T(8,128)} async-done(((f32[768,2880]{1,0:T(8,128)}), f32[192,2880]{1,0:T(8,128)}) %reduce-scatter.2.cloned.1.call-update) | async-done | bytes 2211856 | tf_op jit(solution)/shard_map/reduce_scatter | solution.py:84
  448.7 2.8 convert_element_type.39
  451.5 0.0 all-gather.5.cloned.1.call-update
  451.5 0.1 reshape.244
  451.6 55.4 %all-gather.5.cloned.1.call-done = bf16[768,2880]{1,0:T(8,128)(2,1)} async-done(((bf16[192,2880]{1,0:T(8,128)(2,1)}), bf16[768,2880]{1,0:T(8,128)(2,1)}) %all-gather.5.cloned.1.call-update) | async-done | bytes 4423696 | tf_op jit(solution)/shard_map/all_gather | solution.py:90
  507.0 9.6 %gather_fusion = bf16[512,2880]{1,0:T(8,128)(2,1)} fusion(bf16[768,2880]{1,0:T(8,128)(2,1)} %all-gather.5.cloned.1.call-done, s32[1024]{0:T(1024)S(1)} %pad_clamp_fusion.1), kind=kCustom, calls=%fused_computation | custom fusion | bytes 5900288 | tf_op jit(solution)/shard_map/gather | solution.py:91
  516.6 0.0 copy-start
  516.6 4.7 all-to-all-start.2
  521.3 0.1 add.132
  521.4 0.1 reduce_sum.110
  521.5 0.1 mul.98
  521.6 0.0 copy-done
  521.7 0.1 copy.21
  521.8 68.3 %all-to-all-done.2 = bf16[8,64,2880]{2,1,0:T(8,128)(2,1)S(1)} async-done(((bf16[8,64,2880]{2,1,0:T(8,128)(2,1)}), bf16[8,64,2880]{2,1,0:T(8,128)(2,1)S(1)}, u32[]{:S(2)}, u32[]{:S(2)}) %all-to-all-start.2) | async-done | bytes 2949152 | tf_op jit(solution)/shard_map/all_to_all | solution.py:92
  590.0 1.9 gather_fusion.1
  591.9 1.7 reshape.241
  593.6 1.7 multiply_reduce_fusion
  (11 shorter events, 0.1 us)
Async XLA Ops:
  54.2 9.1 %all-to-all-start = ((s32[8,1,64]{2,1,0:T(1,128)}), s32[8,1,64]{2,1,0:T(1,128)S(1)}, u32[]{:S(2)}, u32[]{:S(2)}) async-start(s32[8,1,64]{2,1,0:T(1,128)} %all_to_all.12), calls=%async_computation | async-start | bytes 8192 | tf_op jit(solution)/shard_map/all_to_all | solution.py:72
  63.3 73.6 %all-to-all-start.1 = ((bf16[8,64,2880]{2,1,0:T(8,128)(2,1)}), bf16[8,64,2880]{2,1,0:T(8,128)(2,1)S(1)}, u32[]{:S(2)}, u32[]{:S(2)}) async-start(bf16[8,64,2880]{2,1,0:T(8,128)(2,1)} %bitcast.6), calls=%async_computation.1 | async-start | bytes 6029312 | tf_op jit(solution)/shard_map/all_to_all | solution.py:71
  68.2 251.5 %all-gather.7.cloned.1.call-start = ((), (), s32[]{:S(2)}) async-start(), calls=%async_computation.6 | async-start | bytes 22609920 | tf_op jit(solution)/shard_map/all_gather | solution.py:79
  151.4 297.3 %reduce-scatter.2.cloned.1.call-start = ((), (), s32[]{:S(2)}) async-start(), calls=%async_computation.4 | async-start | bytes 11304960 | tf_op jit(solution)/shard_map/reduce_scatter | solution.py:84
  356.9 150.1 %all-gather.5.cloned.1.call-start = ((), (), s32[]{:S(2)}) async-start(), calls=%async_computation.5 | async-start | bytes 5652480 | tf_op jit(solution)/shard_map/all_gather | solution.py:90
  516.6 5.1 copy-start
  516.6 73.4 %all-to-all-start.2 = ((bf16[8,64,2880]{2,1,0:T(8,128)(2,1)}), bf16[8,64,2880]{2,1,0:T(8,128)(2,1)S(1)}, u32[]{:S(2)}, u32[]{:S(2)}) async-start(bf16[8,64,2880]{2,1,0:T(8,128)(2,1)} %bitcast.54), calls=%async_computation.3 | async-start | bytes 6029312 | tf_op jit(solution)/shard_map/all_to_all | solution.py:92
Sparse Core Ops, SparseCore 0:
  151.5 168.0 all-gather.6
  357.0 91.6 reduce-scatter.1
  451.6 55.2 all-gather.4
